TPU v7x, 32 devices: a whole 2x2x4 slice. The times are simulated.
32 devices in a mesh: depth: 4 (over z), rows: 8 (over y, x, core).
Axes of the slice: x: 2, y: 2, z: 4, core: 2. Of those that a mesh axis runs over, the one named last changes fastest.
Arguments:
- target: float32 [4, 2, 4096, 4096], P('depth', None, 'rows'), may hold values from -6 to 6
- depth_index: int32 [4], P('depth'), may hold values from 0 to 255
- band_mask: int32 [4, 2, 4096], P('depth'), may hold values from 0 to 1, as said below
Outputs:
- hologram: float32 [2, 4096, 4096], P(None, ('depth', 'rows'))
Inputs may be any that keep to these rules, and one draw needn't show every extreme that they name: `band_mask`: for each plane and each of the two dimensions, the ones are exactly the frequency indices k with min(k, 4096 - k) below a cutoff between 512 and 2048.
All inputs are finite; a program needn't handle non-finite values.
Results may differ from a plain program's by a relative error of at most 0.0009.
Values sent between devices are 32-bit elements; how exact they have to be, the bound alone decides.
A program may use at most 128 MiB of HBM per device.

v0:
```python
import math

import jax
import jax.numpy as jnp
from jax import lax
from jax.sharding import PartitionSpec as P

LOW = 32
HIGH = 128
N = 4096


precise = lax.Precision.HIGHEST


def block_table(length, direction):
    indices = jnp.arange(length, dtype=jnp.int32)
    product = indices[:, None] * indices[None, :] % length
    angles = direction * 2.0 * math.pi / length * product.astype(jnp.float32)
    cosine = jnp.cos(angles)
    sine_part = jnp.sin(angles)
    upper_rows = jnp.stack([cosine, -sine_part], axis=1)
    lower_rows = jnp.stack([sine_part, cosine], axis=1)
    return jnp.stack([upper_rows, lower_rows], axis=0)


def twiddles(direction):
    first = jnp.arange(LOW, dtype=jnp.int32)
    second = jnp.arange(HIGH, dtype=jnp.int32)
    product = first[:, None] * second[None, :] % N
    angles = direction * 2.0 * math.pi / N * product.astype(jnp.float32)
    scaling = 1.0 / math.sqrt(N)
    return (jnp.cos(angles) * scaling, jnp.sin(angles) * scaling)


def rotate_pair(data, factor_real, factor_imaginary, comp_axis):
    real_part = jnp.take(data, 0, axis=comp_axis)
    imaginary_part = jnp.take(data, 1, axis=comp_axis)
    return jnp.stack(
        [
            real_part * factor_real - imaginary_part * factor_imaginary,
            real_part * factor_imaginary + imaginary_part * factor_real,
        ],
        axis=comp_axis,
    )


def along_width(planes):
    plane_count, _, height, _ = planes.shape
    factor_real, factor_imaginary = twiddles(-1.0)
    pieces = planes.reshape(plane_count, 2, height, LOW, HIGH)
    sectioned = jnp.einsum("akbn,pbrnm->parkm", block_table(LOW, -1.0), pieces, precision=precise)
    turned = rotate_pair(sectioned, factor_real, factor_imaginary, 1)
    result = jnp.einsum("akbn,pbrjn->parjk", block_table(HIGH, -1.0), turned, precision=precise)
    return result.reshape(plane_count, 2, height, N)


def along_height(columns):
    plane_count, _, _, slab_width = columns.shape
    factor_real, factor_imaginary = twiddles(-1.0)
    pieces = columns.reshape(plane_count, 2, LOW, HIGH, slab_width)
    sectioned = jnp.einsum("akbn,pbnjs->pakjs", block_table(LOW, -1.0), pieces, precision=precise)
    turned = rotate_pair(sectioned, factor_real[:, :, None], factor_imaginary[:, :, None], 1)
    result = jnp.einsum("akbn,pbjns->pajks", block_table(HIGH, -1.0), turned, precision=precise)
    return result.reshape(plane_count, 2, N, slab_width)


def inverse_height(spectrum):
    slab_width = spectrum.shape[2]
    factor_real, factor_imaginary = twiddles(1.0)
    pieces = spectrum.reshape(2, LOW, HIGH, slab_width)
    sectioned = jnp.einsum("anbk,bjks->ajns", block_table(HIGH, 1.0), pieces, precision=precise)
    turned = rotate_pair(sectioned, factor_real[:, :, None], factor_imaginary[:, :, None], 0)
    result = jnp.einsum("anbk,bkjs->anjs", block_table(LOW, 1.0), turned, precision=precise)
    return result.reshape(2, N, slab_width)


def inverse_width(row_block):
    height = row_block.shape[1]
    factor_real, factor_imaginary = twiddles(1.0)
    pieces = row_block.reshape(2, height, LOW, HIGH)
    sectioned = jnp.einsum("anbk,byjk->ayjn", block_table(HIGH, 1.0), pieces, precision=precise)
    turned = rotate_pair(sectioned, factor_real, factor_imaginary, 0)
    result = jnp.einsum("anbk,bykj->aynj", block_table(LOW, 1.0), turned, precision=precise)
    return result.reshape(2, height, N)


def frequencies(ordering):
    first = ordering // HIGH
    second = ordering % HIGH
    natural = first + LOW * second
    signed = jnp.where(natural < N // 2, natural, natural - N)
    return signed.astype(jnp.float32) / N


def reorder_mask(band_mask):
    leading = band_mask.shape[:-1]
    grid = band_mask.reshape(leading + (HIGH, LOW))
    return jnp.swapaxes(grid, -1, -2).reshape(leading + (N,))


def local(target, depth_index, band_mask):
    plane_count = target.shape[0]
    spectra_width = along_width(target)
    columns = along_height(
        lax.all_to_all(spectra_width, "rows", split_axis=3, concat_axis=2, tiled=True)
    )
    slab_width = columns.shape[3]
    offset = lax.axis_index("rows") * slab_width
    freq_height = frequencies(jnp.arange(N, dtype=jnp.int32))
    freq_width = frequencies(offset + jnp.arange(slab_width, dtype=jnp.int32))
    radical = jnp.sqrt(4.0 - freq_height[:, None] ** 2 - freq_width[None, :] ** 2)
    distance = 100.0 + 2.0 * depth_index.astype(jnp.float32)
    phases = (2.0 * math.pi * distance)[:, None, None] * (radical - 2.0)[None, :, :]
    ordered = reorder_mask(band_mask)
    mask_height = ordered[:, 0, :].astype(jnp.float32)
    mask_width = lax.dynamic_slice_in_dim(ordered[:, 1, :], offset, slab_width, 1).astype(
        jnp.float32
    )
    weights = mask_height[:, :, None] * mask_width[:, None, :]
    cosine = jnp.cos(phases) * weights
    sine_part = jnp.sin(phases) * weights
    real_part = columns[:, 0]
    imaginary_part = columns[:, 1]
    spectrum = jnp.stack(
        [
            jnp.sum(real_part * cosine - imaginary_part * sine_part, axis=0),
            jnp.sum(real_part * sine_part + imaginary_part * cosine, axis=0),
        ]
    )
    scaling = 1.0 / math.sqrt(plane_count * lax.axis_size("depth"))
    field_part = inverse_height(spectrum)
    shares = lax.psum_scatter(field_part, "depth", scatter_dimension=1, tiled=True)
    rows_out = lax.all_to_all(shares, "rows", split_axis=1, concat_axis=2, tiled=True)
    return inverse_width(rows_out) * scaling


def solution(mesh):
    in_specs = (P("depth", None, "rows", None), P("depth"), P("depth", None, None))
    out_specs = P(None, ("depth", "rows"), None)
    return jax.shard_map(local, mesh=mesh, in_specs=in_specs, out_specs=out_specs, check_vma=False)
```

profile of v0, /device:TPU:0, one launch (start us, length us, event | category | flops | bytes accessed | tf_op | source)
XLA Modules:
  0.0 982.7 jit_solution(7739893141141795553)
XLA Ops:
  7.3 14.1 %copy.117 = f32[128,8,32,128]{3,2,1,0:T(8,128)} copy(f32[128,8,32,128]{3,1,2,0:T(8,128)} %bitcast.227) | data formatting | bytes 33554432
  21.4 22.1 %fusion.24 = f32[1,2,512,32,128]{4,3,2,1,0:T(8,128)} fusion(f32[1,32,2,32]{3,1,2,0:T(8,128)S(1)} %get-tuple-element.122, f32[1,32,2,32]{3,1,2,0:T(8,128)S(1)} %get-tuple-element.121, f32[2,512,32,128]{3,2,1,0:T(8,128)} %bitcast.219), kind=kOutput, calls=%fused_computation.39 | convolution fusion | flops 3221229568 | bytes 33570816 | tf_op jit(solution)/shard_map/akbn,pbrnm->parkm/dot_general | solution.py:52
  43.6 7.2 subtract_bitcast_fusion.2
  50.7 6.2 maximum_bitcast_fusion
  56.9 42.9 %fusion.14 = f32[1,2,512,32,128]{2,4,1,3,0:T(8,128)} fusion(f32[2,512,32,128,1]{3,2,1,0,4:T(8,128)} %maximum_bitcast_fusion, f32[1,128,2,128]{3,1,2,0:T(8,128)S(1)} %get-tuple-element.116, f32[1,128,2,128]{3,1,2,0:T(8,128)S(1)} %get-tuple-element.115), kind=kOutput, calls=%fused_computation.20 | convolution fusion | flops 12884967424 | bytes 33816576 | tf_op jit(solution)/shard_map/akbn,pbrjn->parjk/dot_general | solution.py:54
  99.9 6.9 copy.63
  106.7 32.2 %copy.64 = f32[1,2,512,4096]{2,1,0,3:T(2,128)} copy(f32[1,2,512,4096]{2,3,1,0:T(8,128)S(1)} %bitcast.223) | data formatting | bytes 33554432 | tf_op jit(solution)/shard_map/reshape | solution.py:55
  139.0 5.9 all-to-all-start
  146.9 182.5 %all-to-all-done = f32[1,2,512,4096]{2,1,0,3:T(2,128)} async-done(((f32[1,2,512,4096]{2,1,0,3:T(2,128)}), f32[1,2,512,4096]{2,1,0,3:T(2,128)}, u32[]{:S(2)}, u32[]{:S(2)}) %all-to-all-start) | async-done | bytes 16777248 | tf_op jit(solution)/shard_map/all_to_all | solution.py:106
  329.4 14.1 %copy.65 = f32[1,2,512,4096]{2,3,1,0:T(8,128)} copy(f32[1,2,512,4096]{2,1,0,3:T(2,128)} %all-to-all-done) | data formatting | bytes 33554432 | tf_op jit(solution)/shard_map/all_to_all | solution.py:106
  343.5 17.3 %copy.66 = f32[1,2,8,512,512]{4,3,2,1,0:T(8,128)} copy(f32[1,2,8,512,512]{3,4,2,1,0:T(8,128)} %bitcast.224) | data formatting | bytes 33554432 | tf_op jit(solution)/shard_map/all_to_all | solution.py:106
  360.8 32.4 %fusion.17 = f32[1,2,32,128,512]{4,2,1,3,0:T(8,128)S(1)} fusion(f32[2,32,128,512,1]{3,2,1,0,4:T(8,128)} %bitcast.220, f32[1,32,2,32]{3,1,2,0:T(8,128)S(1)} %get-tuple-element.122, f32[1,32,2,32]{3,1,2,0:T(8,128)S(1)} %get-tuple-element.121), kind=kOutput, calls=%fused_computation.21 | convolution fusion | flops 3221229568 | bytes 33570816 | tf_op jit(solution)/shard_map/akbn,pbnjs->pakjs/dot_general | solution.py:62
  402.6 27.0 %fusion.20 = f32[1,2,32,128,512]{4,3,1,2,0:T(8,128)S(1)} fusion(f32[2,32,128,512,1]{3,1,2,0,4:T(8,128)S(1)} %maximum_bitcast_fusion.1, f32[1,128,2,128]{3,1,2,0:T(8,128)S(1)} %get-tuple-element.116, f32[1,128,2,128]{3,1,2,0:T(8,128)S(1)} %get-tuple-element.115), kind=kOutput, calls=%fused_computation.22 | convolution fusion | flops 12884967424 | bytes 33816576 | tf_op jit(solution)/shard_map/akbn,pbjns->pajks/dot_general | solution.py:64
  429.6 6.2 copy.72
  435.8 10.9 %fusion.86 = (f32[1,1,4096,512]{3,2,1,0:T(8,128)}, f32[1,1,4096,512]{3,2,1,0:T(8,128)}) fusion(f32[1,2,4096,512]{3,2,1,0:T(8,128)} %bitcast.222), kind=kLoop, calls=%fused_computation.148 | loop fusion | bytes 33554432 | tf_op jit(solution)/shard_map/slice | solution.py:123
  446.7 9.0 copy.74
  455.7 9.0 copy.75
  464.7 37.7 %multiply_subtract_fusion = (f32[1,32,128,512]{2,3,0,1:T(8,128)S(1)}, f32[1,32,128,512]{2,3,0,1:T(8,128)}) fusion(f32[1,32,128,512]{2,3,0,1:T(8,128)} %copy.75, f32[1,32,128,512]{2,3,0,1:T(8,128)} %copy.74, f32[512]{0:T(512)S(1)} %bitcast.233, f32[32,128]{1,0:T(8,128)S(1)} %bitcast.232, f32[512]{0:T(512)S(1)} %multiply_multiply_fusion.2, ...), kind=kLoop, calls=%fused_computation.33 | loop fusion | flops 25165824 | bytes 33591300 | tf_op jit(solution)/shard_map/sub | solution.py:127
  502.4 16.5 %fusion.23 = f32[2,32,128,512]{2,3,0,1:T(8,128)S(1)} fusion(f32[1,32,128,512]{2,3,0,1:T(8,128)} %get-tuple-element.104, f32[1,32,128,512]{2,3,0,1:T(8,128)S(1)} %get-tuple-element.103, f32[1,128,2,128]{3,1,2,0:T(8,128)S(1)} %get-tuple-element.114, f32[1,128,2,128]{3,1,2,0:T(8,128)S(1)} %get-tuple-element.113), kind=kOutput, calls=%fused_computation.23 | convolution fusion | flops 12889161728 | bytes 33816576 | tf_op jit(solution)/shard_map/anbk,bjks->ajns/dot_general | solution.py:72
  518.9 6.9 subtract_bitcast_fusion
  525.8 11.5 %pad_maximum_fusion = f32[2,32,128,512]{2,3,1,0:T(8,128)} fusion(f32[1,32,128,512]{2,3,1,0:T(8,128)} %get-tuple-element.106, f32[1,32,128,512]{2,3,1,0:T(8,128)} %get-tuple-element.105), kind=kLoop, calls=%fused_computation.6 | loop fusion | flops 4194304 | bytes 33554432 | tf_op jit(solution)/shard_map/stack | solution.py:39
  537.3 19.9 %copy.79 = f32[2,32,128,512]{3,1,0,2:T(8,128)} copy(f32[2,32,128,512]{2,3,1,0:T(8,128)} %pad_maximum_fusion) | data formatting | bytes 33554432 | tf_op jit(solution)/shard_map/stack | solution.py:39
  557.2 21.8 %fusion.27 = f32[2,32,128,512]{3,1,2,0:T(8,128)} fusion(f32[2,32,128,512]{3,1,0,2:T(8,128)} %copy.79, f32[1,32,2,32]{3,1,2,0:T(8,128)S(1)} %get-tuple-element.120, f32[1,32,2,32]{3,1,2,0:T(8,128)S(1)} %get-tuple-element.119), kind=kOutput, calls=%fused_computation.40 | convolution fusion | flops 3221229568 | bytes 33570816 | tf_op jit(solution)/shard_map/anbk,bkjs->anjs/dot_general | solution.py:74
  579.0 17.9 %copy.80 = f32[2,32,128,512]{3,2,1,0:T(8,128)} copy(f32[2,32,128,512]{3,1,2,0:T(8,128)} %fusion.27) | data formatting | bytes 33554432 | tf_op jit(solution)/shard_map/anbk,bkjs->anjs/dot_general | solution.py:74
  596.9 280.8 %reduce-scatter.2.cloned.1.call-done = f32[2,1024,512]{2,1,0:T(8,128)} async-done(((f32[2,4096,512]{2,1,0:T(8,128)}), f32[2,1024,512]{2,1,0:T(8,128)}) %reduce-scatter.2.cloned.1.call-update) | async-done | bytes 4194320 | tf_op jit(solution)/shard_map/reduce_scatter | solution.py:133
  877.7 5.4 copy.81
  883.1 52.5 %all_to_all.30 = f32[2,1024,512]{2,0,1:T(2,128)S(1)} all-to-all(f32[2,1024,512]{2,0,1:T(2,128)S(1)} %copy.81), channel_id=1, replica_groups=mesh['depth'=4,'rows'=8] {'rows'}, dimensions={1} | all-to-all | bytes 8388608 | tf_op jit(solution)/shard_map/all_to_all | solution.py:134
  938.4 5.3 copy.83
  943.8 8.5 fusion.35
  953.7 9.0 fusion.30
  962.7 6.0 mul.976
  968.8 6.6 copy.87
  (31 shorter events, 15.7 us)
Async XLA Ops:
  139.0 6.1 copy-start
  139.0 190.5 %all-to-all-start = ((f32[1,2,512,4096]{2,1,0,3:T(2,128)}), f32[1,2,512,4096]{2,1,0,3:T(2,128)}, u32[]{:S(2)}, u32[]{:S(2)}) async-start(f32[1,2,512,4096]{2,1,0,3:T(2,128)} %copy.64), calls=%async_computation | async-start | bytes 33554432 | tf_op jit(solution)/shard_map/all_to_all | solution.py:106
  144.9 732.9 %reduce-scatter.2.cloned.1.call-start = ((), (), s32[]{:S(2)}) async-start(), calls=%async_computation.3 | async-start | bytes 20971520 | tf_op jit(solution)/shard_map/reduce_scatter | solution.py:133
Sparse Core Ops, SparseCore 0:
  597.0 280.6 reduce-scatter.1
where the time goes:
time: 993 us; the launch traced here: 983 us
  waiting for transfers between devices  463 us (47%)
  local copies, waits for them, and re-layouts  184 us (19%)
  matrix products  180 us (18%)
  other arithmetic  81.9 us (8%)
  blocking collectives  52.5 us (5%)
  between operations  14.7 us (1%)
    reduce_scatter x1, waiting for transfers between devices, local(): lax.psum_scatter(field_part, 'depth', scatter_dimension=1, tiled=True)  281 us
    all_to_all x1, waiting for transfers between devices, local(): lax.all_to_all(spectra_width, 'rows', split_axis=3, concat_axis=2, tiled=...  183 us
    all_to_all x1, blocking collectives, local(): lax.all_to_all(shares, 'rows', split_axis=1, concat_axis=2, tiled=True)  52.5 us
    dot_general x1, matrix products, along_width(): jnp.einsum('akbn,pbrjn->parjk', block_table(HIGH, -1.0), turned, precisio...  42.9 us
    sub x1, other arithmetic, local(): real_part * cosine - imaginary_part * sine_part  37.7 us
    dot_general x1, matrix products, along_height(): jnp.einsum('akbn,pbnjs->pakjs', block_table(LOW, -1.0), pieces, precision...  32.4 us
    reshape x1, local copies, waits for them, and re-layouts, along_width(): return result.reshape(plane_count, 2, height, N)  32.2 us
    another operation x6, other arithmetic, rotate_pair(): jnp.stack([real_part * factor_real - imaginary_part * factor_imaginary, r...  31.4 us
  transfers between devices with their start and end apart: 2, of which 2 were waited for; matrix products, arithmetic and copies ran while one was open for 0% of the time, Pallas kernels for 0%

commit v1 on v0

v1 whole, which is shorter than its diff:
```python
import functools
import math

import jax
import jax.numpy as jnp
import numpy as np
from jax import lax
from jax.experimental import pallas as pl
from jax.experimental.pallas import tpu as pltpu
from jax.sharding import PartitionSpec as P

LOW = 32
HIGH = 128
N = LOW * HIGH
VMEM_LIMIT = 56 * 1024 * 1024


def scaled(value, factor_real, factor_imaginary):
    real, imaginary = value
    if abs(factor_imaginary) < 1e-12:
        if factor_real > 0:
            return (real, imaginary)
        return (-real, -imaginary)
    if abs(factor_real) < 1e-12:
        if factor_imaginary > 0:
            return (-imaginary, real)
        return (imaginary, -real)
    a, b = np.float32(factor_real), np.float32(factor_imaginary)
    return (real * a - imaginary * b, real * b + imaginary * a)


def root(numerator, length, direction):
    angle = direction * 2.0 * math.pi * (numerator % length) / length
    return math.cos(angle), math.sin(angle)


def add(left, right):
    return (left[0] + right[0], left[1] + right[1])


def subtract(left, right):
    return (left[0] - right[0], left[1] - right[1])


def butterfly(values, direction):
    count = len(values)
    if count == 1:
        return values
    even = butterfly(values[0::2], direction)
    odd = butterfly(values[1::2], direction)
    odd = [scaled(v, *root(k, count, direction)) for k, v in enumerate(odd)]
    return [add(e, o) for e, o in zip(even, odd)] + [subtract(e, o) for e, o in zip(even, odd)]


def dense_table(direction):
    index = np.arange(HIGH)
    angles = direction * 2.0 * np.pi / HIGH * (index[:, None] * index[None, :] % HIGH)
    cosine, sine = np.cos(angles), np.sin(angles)
    return np.block([[cosine, -sine], [sine, cosine]])


def halves(table):
    high = table.astype(np.float32).astype(jnp.bfloat16)
    low = (table - high.astype(np.float64)).astype(np.float32).astype(jnp.bfloat16)
    return jnp.asarray(high), jnp.asarray(low)


def twiddles(direction, scaling):
    product = np.arange(LOW)[:, None] * np.arange(HIGH)[None, :] % N
    angles = direction * 2.0 * np.pi / N * product
    return (
        jnp.asarray((np.cos(angles) * scaling).astype(np.float32)),
        jnp.asarray((np.sin(angles) * scaling).astype(np.float32)),
    )


def split(value):
    high = value.astype(jnp.bfloat16)
    return high, (value - high.astype(jnp.float32)).astype(jnp.bfloat16)


def dot(left, right):
    return jnp.dot(left, right, preferred_element_type=jnp.float32)


def width_kernel(chunk, chunks, owners, x_ref, tr_ref, ti_ref, th_ref, tl_ref, o_ref, hi_ref, lo_ref):
    tile = x_ref.shape[1]

    def body(step, carry):
        rows = pl.ds(pl.multiple_of(step * 16, 16), 16)
        values = []
        for first in range(owners):
            total = None
            for second in range(chunks):
                at = (first + owners * second) * HIGH
                value = (x_ref[0, rows, at:at + HIGH], x_ref[1, rows, at:at + HIGH])
                value = scaled(value, *root(chunk * second, chunks, -1.0))
                total = value if total is None else add(total, value)
            values.append(scaled(total, *root(chunk * first, LOW, -1.0)))
        for owner, (real, imaginary) in enumerate(butterfly(values, -1.0)):
            k = chunks * owner + chunk
            turn_real, turn_imaginary = tr_ref[k:k + 1, :], ti_ref[k:k + 1, :]
            high, low = split(real * turn_real - imaginary * turn_imaginary)
            hi_ref[owner, rows, :HIGH] = high
            lo_ref[owner, rows, :HIGH] = low
            high, low = split(real * turn_imaginary + imaginary * turn_real)
            hi_ref[owner, rows, HIGH:] = high
            lo_ref[owner, rows, HIGH:] = low
        return carry

    lax.fori_loop(0, tile // 16, body, 0)
    for owner in range(owners):
        high = hi_ref[owner]
        out = dot(high, th_ref[...]) + dot(lo_ref[owner], th_ref[...]) + dot(high, tl_ref[...])
        o_ref[owner, 0] = out[:, :HIGH]
        o_ref[owner, 1] = out[:, HIGH:]


def along_width(field, chunk, chunks, owners, tables):
    _, height, _ = field.shape
    tile = min(128, height)
    whole = lambda a: pl.BlockSpec(a.shape, lambda i: (0,) * a.ndim)
    return pl.pallas_call(
        functools.partial(width_kernel, chunk, chunks, owners),
        grid=(height // tile,),
        in_specs=[pl.BlockSpec((2, tile, N), lambda i: (0, i, 0))] + [whole(a) for a in tables],
        out_specs=pl.BlockSpec((owners, 2, tile, HIGH), lambda i: (0, 0, i, 0)),
        out_shape=jax.ShapeDtypeStruct((owners, 2, height, HIGH), jnp.float32),
        scratch_shapes=[pltpu.VMEM((owners, tile, 2 * HIGH), jnp.bfloat16)] * 2,
        compiler_params=pltpu.CompilerParams(vmem_limit_bytes=VMEM_LIMIT),
        cost_estimate=pl.CostEstimate(flops=6 * height * HIGH * HIGH * 4 * owners * 2, bytes_accessed=field.size * 4 + field.size * 4 // chunks, transcendentals=0),
        name=f"width_{chunk}",
    )(field, *tables)


def series(values, points):
    nodes = np.cos(np.pi * (np.arange(400) + 0.5) / 400) * 0.125 + 0.125
    basis = np.polynomial.chebyshev.Chebyshev.fit(nodes, values(np.sqrt(nodes)), points, domain=[0.0, 0.25])
    return [np.float32(c) for c in basis.convert(kind=np.polynomial.Polynomial).coef]


COSINE = series(lambda r: np.cos(2.0 * np.pi * r), 8)
SINE = series(lambda r: np.sin(2.0 * np.pi * r) / r, 8)


def horner(coefficients, at):
    total = coefficients[-1]
    for c in coefficients[-2::-1]:
        total = total * at + c
    return total


def signed(natural):
    return jnp.where(natural < N // 2, natural, natural - N).astype(jnp.float32)


def column_kernel(scalars_ref, x_ref, tr_ref, ti_ref, fh_ref, fl_ref, ih_ref, il_ref, o_ref, work_ref):
    owners, _, pieces, _, _ = x_ref.shape
    distance = scalars_ref[0].astype(jnp.float32) * 2.0 + 100.0
    limit_height = scalars_ref[1].astype(jnp.float32)
    limit_width = scalars_ref[2].astype(jnp.float32)
    column = scalars_ref[3]

    def forward(step, carry):
        rows = pl.ds(pl.multiple_of(step * 8, 8), 8)
        low_rows = pl.ds(pl.multiple_of(step * 8 + HIGH, 8), 8)
        values = [(x_ref[s, 0, p, rows, :], x_ref[s, 1, p, rows, :]) for s in range(owners) for p in range(pieces)]
        for k, (real, imaginary) in enumerate(butterfly(values, -1.0)):
            work_ref[k, rows, :] = real
            work_ref[k, low_rows, :] = imaginary
        return carry

    lax.fori_loop(0, HIGH // 8, forward, 0)

    across = signed(lax.broadcasted_iota(jnp.int32, (1, HIGH), 1) * LOW + column)
    inside_width = jnp.abs(across) < limit_width
    across_square = (across * (1.0 / N)) ** 2

    def turned(k, sign):
        real, imaginary = work_ref[k, :HIGH, :], work_ref[k, HIGH:, :]
        turn_real, turn_imaginary = tr_ref[k], ti_ref[k]
        return jnp.concatenate(
            [real * turn_real - imaginary * turn_imaginary, real * turn_imaginary + imaginary * turn_real], axis=0
        )

    def propagate(k, real, imaginary):
        down = signed(lax.broadcasted_iota(jnp.int32, (HIGH, HIGH), 0) * LOW + k)
        square = (down * (1.0 / N)) ** 2 + across_square
        turns = -distance * (square / (jnp.sqrt(4.0 - square) + 2.0))
        rest = turns - jnp.floor(turns + 0.5)
        at = rest * rest
        keep = jnp.logical_and(jnp.abs(down) < limit_height, inside_width)
        cosine = jnp.where(keep, horner(COSINE, at), 0.0)
        sine = jnp.where(keep, horner(SINE, at) * rest, 0.0)
        return jnp.concatenate([real * cosine - imaginary * sine, real * sine + imaginary * cosine], axis=0)

    def middle(step, carry):
        pair = [2 * step, 2 * step + 1]
        high, low = split(jnp.concatenate([turned(k, 1.0) for k in pair], axis=1))
        spectrum = dot(fh_ref[...], high) + dot(fh_ref[...], low) + dot(fl_ref[...], high)
        moved = [
            propagate(k, spectrum[:HIGH, i * HIGH:(i + 1) * HIGH], spectrum[HIGH:, i * HIGH:(i + 1) * HIGH])
            for i, k in enumerate(pair)
        ]
        high, low = split(jnp.concatenate(moved, axis=1))
        back = dot(ih_ref[...], high) + dot(ih_ref[...], low) + dot(il_ref[...], high)
        for i, k in enumerate(pair):
            real, imaginary = back[:HIGH, i * HIGH:(i + 1) * HIGH], back[HIGH:, i * HIGH:(i + 1) * HIGH]
            turn_real, turn_imaginary = tr_ref[k], ti_ref[k]
            work_ref[k, :HIGH, :] = real * turn_real + imaginary * turn_imaginary
            work_ref[k, HIGH:, :] = imaginary * turn_real - real * turn_imaginary
        return carry

    lax.fori_loop(0, LOW // 2, middle, 0)

    def inverse(step, carry):
        rows = pl.ds(pl.multiple_of(step * 8, 8), 8)
        low_rows = pl.ds(pl.multiple_of(step * 8 + HIGH, 8), 8)
        values = [(work_ref[k, rows, :], work_ref[k, low_rows, :]) for k in range(LOW)]
        for j, (real, imaginary) in enumerate(butterfly(values, 1.0)):
            o_ref[j, 0, rows, :] = real
            o_ref[j, 1, rows, :] = imaginary
        return carry

    lax.fori_loop(0, HIGH // 8, inverse, 0)


def columns_step(received, scalars, tables, chunk):
    owners, _, height, _ = received.shape
    received = received.reshape(owners, 2, height // HIGH, HIGH, HIGH)
    vmem = pl.BlockSpec(memory_space=pltpu.VMEM)
    return pl.pallas_call(
        column_kernel,
        in_specs=[pl.BlockSpec(memory_space=pltpu.SMEM)] + [vmem] * (1 + len(tables)),
        out_specs=vmem,
        out_shape=jax.ShapeDtypeStruct((LOW, 2, HIGH, HIGH), jnp.float32),
        scratch_shapes=[pltpu.VMEM((LOW, 2 * HIGH, HIGH), jnp.float32)],
        compiler_params=pltpu.CompilerParams(vmem_limit_bytes=VMEM_LIMIT),
        cost_estimate=pl.CostEstimate(flops=12 * LOW * HIGH * 256 * 256 * 2, bytes_accessed=16 * 1024 * 1024, transcendentals=0),
        name=f"column_{chunk}",
    )(scalars, received, *tables)


def output_kernel(chunks, *refs):
    inputs = refs[:chunks]
    tr_ref, ti_ref, th_ref, tl_ref, o_ref, work_ref = refs[chunks:]
    owners, _, height, _ = inputs[0].shape
    for owner in range(owners):
        for chunk in range(chunks):
            k = chunks * owner + chunk
            value = jnp.concatenate([inputs[chunk][owner, 0], inputs[chunk][owner, 1]], axis=1)
            high, low = split(value)
            out = dot(high, th_ref[...]) + dot(low, th_ref[...]) + dot(high, tl_ref[...])
            real, imaginary = out[:, :HIGH], out[:, HIGH:]
            turn_real, turn_imaginary = tr_ref[k:k + 1, :], ti_ref[k:k + 1, :]
            work_ref[k, 0] = real * turn_real - imaginary * turn_imaginary
            work_ref[k, 1] = real * turn_imaginary + imaginary * turn_real

    def body(step, carry):
        rows = pl.ds(pl.multiple_of(step * 8, 8), 8)
        values = [(work_ref[k, 0, rows, :], work_ref[k, 1, rows, :]) for k in range(LOW)]
        for j, (real, imaginary) in enumerate(butterfly(values, 1.0)):
            o_ref[0, rows, j * HIGH:(j + 1) * HIGH] = real
            o_ref[1, rows, j * HIGH:(j + 1) * HIGH] = imaginary
        return carry

    lax.fori_loop(0, height // 8, body, 0)


def inverse_width(parts, tables):
    height = parts[0].shape[2]
    vmem = pl.BlockSpec(memory_space=pltpu.VMEM)
    return pl.pallas_call(
        functools.partial(output_kernel, len(parts)),
        in_specs=[vmem] * (len(parts) + len(tables)),
        out_specs=vmem,
        out_shape=jax.ShapeDtypeStruct((2, height, N), jnp.float32),
        scratch_shapes=[pltpu.VMEM((LOW, 2, height, HIGH), jnp.float32)],
        compiler_params=pltpu.CompilerParams(vmem_limit_bytes=VMEM_LIMIT),
        cost_estimate=pl.CostEstimate(flops=6 * LOW * height * 256 * 256, bytes_accessed=8 * height * N * 2, transcendentals=0),
        name="output",
    )(*parts, *tables)


def local(target, depth_index, band_mask):
    owners, depths = lax.axis_size("rows"), lax.axis_size("depth")
    chunks = LOW // owners
    field = target.reshape(target.shape[1:])
    scale = 1.0 / math.sqrt(N)
    forward, backward = dense_table(-1.0), dense_table(1.0)
    forward_left, backward_left = halves(forward), halves(backward)
    forward_right, backward_right = halves(forward.T), halves(backward.T)
    turn = twiddles(-1.0, scale)
    turn_back = twiddles(1.0, scale / math.sqrt(depths))
    spread = tuple(jnp.broadcast_to(t[:, :, None], (LOW, HIGH, HIGH)) for t in turn)
    limits = (jnp.sum(band_mask[0], axis=-1) + 1) // 2
    me = lax.axis_index("rows")
    rows = N // (owners * depths)

    pieces = []
    for chunk in range(chunks):
        sent = along_width(field, chunk, chunks, owners, turn + forward_right)
        received = lax.all_to_all(sent, "rows", split_axis=0, concat_axis=0, tiled=True)
        scalars = jnp.stack([depth_index[0], limits[0], limits[1], me * chunks + chunk]).astype(jnp.int32)
        part = columns_step(received, scalars, spread + forward_left + backward_left, chunk)
        pieces.append(lax.psum_scatter(part, "depth", scatter_dimension=0, tiled=True))
    results = []
    for share in pieces:
        share = share.reshape(share.shape[0], 2, HIGH // rows, rows, HIGH)
        share = jnp.transpose(share, (0, 2, 1, 3, 4)).reshape(owners, 2, rows, HIGH)
        results.append(lax.all_to_all(share, "rows", split_axis=0, concat_axis=0, tiled=True))
    return inverse_width(results, turn_back + backward_right)


def solution(mesh):
    in_specs = (P("depth", None, "rows", None), P("depth"), P("depth", None, None))
    out_specs = P(None, ("depth", "rows"), None)
    return jax.shard_map(local, mesh=mesh, in_specs=in_specs, out_specs=out_specs, check_vma=False)
```

time: 993 us -> 472 us (0.48)
  waiting for transfers between devices: 463 us -> 162 us
  local copies, waits for them, and re-layouts: 184 us -> 3.88 us
  matrix products: 180 us -> 0 us
  Pallas kernels: 0 us -> 143 us
  other arithmetic: 81.9 us -> 1.47 us
  blocking collectives: 52.5 us -> 127 us
  starting transfers between devices: 5.92 us -> 20.8 us
    reduce_scatter x1 -> x4, waiting for transfers between devices: 281 us -> 35.2 us  [local(): lax.psum_scatter(part, 'depth', scatter_dimension=0, tiled=True)]
    dot_general x8 -> x0, matrix products: 180 us -> none  [the longest x1 42.9 us: along_width(): jnp.einsum('akbn,pbrjn->parjk', block_table(HIGH, -1.0), turned, precisio...]
    pallas_call x0 -> x9, Pallas kernels: none -> 143 us  [the longest x4 92.9 us: columns_step(): pl.pallas_call(column_kernel, in_specs=[pl.BlockSpec(memory_space=pltpu.S...]
    all_to_all x1 -> x3, blocking collectives: 52.5 us -> 127 us  [the longest x2 107 us: local(): lax.all_to_all(sent, 'rows', split_axis=0, concat_axis=0, tiled=True)]
    all_to_all x1 -> x5, waiting for transfers between devices: 183 us -> 127 us  [the longest x2 96.1 us: local(): lax.all_to_all(sent, 'rows', split_axis=0, concat_axis=0, tiled=True)]
    another operation x12 -> x2, other arithmetic: 42.5 us -> 1.3 us  [local(): jnp.stack([depth_index[0], limits[0], limits[1], me * chunks + chunk])]
    all_to_all x4 -> x0, local copies, waits for them, and re-layouts: 39.5 us -> none  [the longest x2 31.4 us: local(): lax.all_to_all(spectra_width, 'rows', split_axis=3, concat_axis=2, tiled=...]
    sub x2 -> x0, other arithmetic: 37.7 us -> none  [the longest x1 37.7 us: local(): real_part * cosine - imaginary_part * sine_part]
  transfers between devices with their start and end apart: 2 -> 9, of which waited for: 2 -> 5; matrix products, arithmetic and copies ran while one was open for 0% -> 0% of each run, Pallas kernels for 0% -> 22%
where the time goes in v1:
time: 472 us; the launch traced here: 471 us
  waiting for transfers between devices  162 us (34%)
  Pallas kernels  143 us (30%)
  blocking collectives  127 us (27%)
  starting transfers between devices  20.8 us (4%)
  between operations  13.9 us (3%)
    all_to_all x2, blocking collectives, local(): lax.all_to_all(sent, 'rows', split_axis=0, concat_axis=0, tiled=True)  107 us
    all_to_all x2, waiting for transfers between devices, local(): lax.all_to_all(sent, 'rows', split_axis=0, concat_axis=0, tiled=True)  96.1 us
    pallas_call x4, Pallas kernels, columns_step(): pl.pallas_call(column_kernel, in_specs=[pl.BlockSpec(memory_space=pltpu.S...  92.9 us
    pallas_call x4, Pallas kernels, along_width(): pl.pallas_call(functools.partial(width_kernel, chunk, chunks, owners), gr...  41.8 us
    reduce_scatter x4, waiting for transfers between devices, local(): lax.psum_scatter(part, 'depth', scatter_dimension=0, tiled=True)  35.2 us
    all_to_all x3, waiting for transfers between devices, local(): lax.all_to_all(share, 'rows', split_axis=0, concat_axis=0, tiled=True)  30.6 us
    all_to_all x1, blocking collectives, local(): lax.all_to_all(share, 'rows', split_axis=0, concat_axis=0, tiled=True)  19.6 us
    all_to_all x3, starting transfers between devices, local(): lax.all_to_all(share, 'rows', split_axis=0, concat_axis=0, tiled=True)  10.7 us
  transfers between devices with their start and end apart: 9, of which 5 were waited for; matrix products, arithmetic and copies ran while one was open for 0% of the time, Pallas kernels for 22%

profile of v1, /device:TPU:0, one launch (start us, length us, event | category | flops | bytes accessed | tf_op | source)
XLA Modules:
  0.0 471.1 jit_solution(2292124250936452430)
XLA Ops:
  6.5 10.1 %width_3.1 = f32[8,2,512,128]{3,2,1,0:T(8,128)} custom-call(f32[2,512,4096]{2,1,0:T(8,128)} %bitcast.9, f32[32,128]{1,0:T(8,128)} %constant.46.clone.tr_ref, f32[32,128]{1,0:T(8,128)} %constant.47.clone.ti_ref, bf16[256,256]{1,0:T(8,128)(2,1)} %constant.44.clone.th_ref.ih_ref, bf16[256,256]{1,0:T(8,128)(2,1)} %constant.45.clone.tl_ref.il_ref), custom_call_target="tpu_custom_call" | custom-call | flops 3221225472 | bytes 20971520 | tf_op jit(solution)/shard_map/width_3/pallas_call | solution.py:123
  16.6 5.3 %all-to-all-start.6 = ((f32[8,2,512,128]{3,2,1,0:T(8,128)}), f32[8,2,512,128]{3,2,1,0:T(8,128)}, u32[]{:S(2)}, u32[]{:S(2)}) async-start(f32[8,2,512,128]{3,2,1,0:T(8,128)} %width_3.1), calls=%async_computation.9 | async-start | bytes 8388608 | tf_op jit(solution)/shard_map/all_to_all | solution.py:303
  22.0 0.0 reduce-scatter.11.cloned.1.call-start
  22.7 0.2 reduce_sum.9
  22.8 0.7 pad_add_fusion.4
  23.5 47.7 %all-to-all-done.6 = f32[8,2,512,128]{3,2,1,0:T(8,128)} async-done(((f32[8,2,512,128]{3,2,1,0:T(8,128)}), f32[8,2,512,128]{3,2,1,0:T(8,128)}, u32[]{:S(2)}, u32[]{:S(2)}) %all-to-all-start.6) | async-done | bytes 4194336 | tf_op jit(solution)/shard_map/all_to_all | solution.py:303
  71.2 1.9 broadcast_in_dim.4.tr_ref
  73.1 1.9 broadcast_in_dim.5.ti_ref
  75.0 23.1 %column_3.1 = f32[32,2,128,128]{3,2,1,0:T(8,128)} custom-call(s32[4]{0:T(128)} %get-tuple-element.5.scalars_ref, f32[8,2,4,128,128]{4,3,2,1,0:T(8,128)} %bitcast.8.x_ref, f32[32,128,128]{2,1,0:T(8,128)} %broadcast_in_dim.4.tr_ref, f32[32,128,128]{2,1,0:T(8,128)} %broadcast_in_dim.5.ti_ref, bf16[256,256]{1,0:T(8,128)(2,1)} %constant.42.clone.fh_ref.refs_6_, ...), custom_call_target="tpu_custom_call" | custom-call | flops 6442450944 | bytes 16777216 | tf_op jit(solution)/shard_map/column_3/pallas_call | solution.py:232
  98.2 10.8 %width_2.1 = f32[8,2,512,128]{3,2,1,0:T(8,128)} custom-call(f32[2,512,4096]{2,1,0:T(8,128)} %bitcast.10, f32[32,128]{1,0:T(8,128)} %constant.46.clone.tr_ref, f32[32,128]{1,0:T(8,128)} %constant.47.clone.ti_ref, bf16[256,256]{1,0:T(8,128)(2,1)} %constant.44.clone.th_ref.ih_ref, bf16[256,256]{1,0:T(8,128)(2,1)} %constant.45.clone.tl_ref.il_ref), custom_call_target="tpu_custom_call" | custom-call | flops 3221225472 | bytes 20971520 | tf_op jit(solution)/shard_map/width_2/pallas_call | solution.py:123
  109.0 4.6 all-to-all-start.4
  113.6 0.0 reduce-scatter.9.cloned.1.call-start
  113.6 0.7 pad_add_fusion.3
  114.3 48.4 %all-to-all-done.4 = f32[8,2,512,128]{3,2,1,0:T(8,128)} async-done(((f32[8,2,512,128]{3,2,1,0:T(8,128)}), f32[8,2,512,128]{3,2,1,0:T(8,128)}, u32[]{:S(2)}, u32[]{:S(2)}) %all-to-all-start.4) | async-done | bytes 4194336 | tf_op jit(solution)/shard_map/all_to_all | solution.py:303
  162.7 23.2 %column_2.1 = f32[32,2,128,128]{3,2,1,0:T(8,128)} custom-call(s32[4]{0:T(128)} %get-tuple-element.7.scalars_ref, f32[8,2,4,128,128]{4,3,2,1,0:T(8,128)} %bitcast.6.x_ref, f32[32,128,128]{2,1,0:T(8,128)} %broadcast_in_dim.4.tr_ref, f32[32,128,128]{2,1,0:T(8,128)} %broadcast_in_dim.5.ti_ref, bf16[256,256]{1,0:T(8,128)(2,1)} %constant.42.clone.fh_ref.refs_6_, ...), custom_call_target="tpu_custom_call" | custom-call | flops 6442450944 | bytes 16777216 | tf_op jit(solution)/shard_map/column_2/pallas_call | solution.py:232
  185.9 0.0 reduce-scatter.7.cloned.1.call-start
  186.0 10.6 %width_1.1 = f32[8,2,512,128]{3,2,1,0:T(8,128)} custom-call(f32[2,512,4096]{2,1,0:T(8,128)} %bitcast.11, f32[32,128]{1,0:T(8,128)} %constant.46.clone.tr_ref, f32[32,128]{1,0:T(8,128)} %constant.47.clone.ti_ref, bf16[256,256]{1,0:T(8,128)(2,1)} %constant.44.clone.th_ref.ih_ref, bf16[256,256]{1,0:T(8,128)(2,1)} %constant.45.clone.tl_ref.il_ref), custom_call_target="tpu_custom_call" | custom-call | flops 3221225472 | bytes 20971520 | tf_op jit(solution)/shard_map/width_1/pallas_call | solution.py:123
  196.6 53.5 %all_to_all.40 = f32[8,2,512,128]{3,2,1,0:T(8,128)} all-to-all(f32[8,2,512,128]{3,2,1,0:T(8,128)} %width_1.1), channel_id=1, replica_groups=mesh['depth'=4,'rows'=8] {'rows'}, dimensions={0} | all-to-all | bytes 8388608 | tf_op jit(solution)/shard_map/all_to_all | solution.py:303
  250.2 23.2 %column_1.1 = f32[32,2,128,128]{3,2,1,0:T(8,128)} custom-call(s32[4]{0:T(128)} %get-tuple-element.8.scalars_ref, f32[8,2,4,128,128]{4,3,2,1,0:T(8,128)} %bitcast.14, f32[32,128,128]{2,1,0:T(8,128)} %broadcast_in_dim.4.tr_ref, f32[32,128,128]{2,1,0:T(8,128)} %broadcast_in_dim.5.ti_ref, bf16[256,256]{1,0:T(8,128)(2,1)} %constant.42.clone.fh_ref.refs_6_, ...), custom_call_target="tpu_custom_call" | custom-call | flops 6442450944 | bytes 16777216 | tf_op jit(solution)/shard_map/column_1/pallas_call | solution.py:232
  273.4 0.0 reduce-scatter.5.cloned.1.call-start
  273.5 10.3 %width_0.1 = f32[8,2,512,128]{3,2,1,0:T(8,128)} custom-call(f32[2,512,4096]{2,1,0:T(8,128)} %bitcast.12, f32[32,128]{1,0:T(8,128)} %constant.46.clone.tr_ref, f32[32,128]{1,0:T(8,128)} %constant.47.clone.ti_ref, bf16[256,256]{1,0:T(8,128)(2,1)} %constant.44.clone.th_ref.ih_ref, bf16[256,256]{1,0:T(8,128)(2,1)} %constant.45.clone.tl_ref.il_ref), custom_call_target="tpu_custom_call" | custom-call | flops 3221225472 | bytes 20971520 | tf_op jit(solution)/shard_map/width_0/pallas_call | solution.py:123
  283.8 53.5 %all_to_all.41 = f32[8,2,512,128]{3,2,1,0:T(8,128)} all-to-all(f32[8,2,512,128]{3,2,1,0:T(8,128)} %width_0.1), channel_id=1, replica_groups=mesh['depth'=4,'rows'=8] {'rows'}, dimensions={0} | all-to-all | bytes 8388608 | tf_op jit(solution)/shard_map/all_to_all | solution.py:303
  337.4 23.3 %column_0.1 = f32[32,2,128,128]{3,2,1,0:T(8,128)} custom-call(s32[4]{0:T(128)} %get-tuple-element.9.scalars_ref, f32[8,2,4,128,128]{4,3,2,1,0:T(8,128)} %bitcast.13, f32[32,128,128]{2,1,0:T(8,128)} %broadcast_in_dim.4.tr_ref, f32[32,128,128]{2,1,0:T(8,128)} %broadcast_in_dim.5.ti_ref, bf16[256,256]{1,0:T(8,128)(2,1)} %constant.42.clone.fh_ref.refs_6_, ...), custom_call_target="tpu_custom_call" | custom-call | flops 6442450944 | bytes 16777216 | tf_op jit(solution)/shard_map/column_0/pallas_call | solution.py:232
  360.7 3.6 all-to-all-start.7
  364.3 0.0 reduce-scatter.9.cloned.1.call-done
  364.3 15.3 %all-to-all-done.7.refs_3_ = f32[8,2,128,128]{3,2,1,0:T(8,128)S(1)} async-done(((f32[8,2,128,128]{3,2,1,0:T(8,128)}), f32[8,2,128,128]{3,2,1,0:T(8,128)S(1)}, u32[]{:S(2)}, u32[]{:S(2)}) %all-to-all-start.7) | async-done | bytes 1048608 | tf_op jit(solution)/shard_map/all_to_all | solution.py:311
  379.6 3.6 all-to-all-start.5
  383.2 15.3 %all-to-all-done.5.refs_2_ = f32[8,2,128,128]{3,2,1,0:T(8,128)S(1)} async-done(((f32[8,2,128,128]{3,2,1,0:T(8,128)}), f32[8,2,128,128]{3,2,1,0:T(8,128)S(1)}, u32[]{:S(2)}, u32[]{:S(2)}) %all-to-all-start.5) | async-done | bytes 1048608 | tf_op jit(solution)/shard_map/all_to_all | solution.py:311
  398.5 3.6 all-to-all-start.3
  402.1 35.1 %reduce-scatter.5.cloned.1.call-done = f32[8,2,128,128]{3,2,1,0:T(8,128)} async-done(((f32[32,2,128,128]{3,2,1,0:T(8,128)}), f32[8,2,128,128]{3,2,1,0:T(8,128)}) %reduce-scatter.5.cloned.1.call-update) | async-done | bytes 1048592 | tf_op jit(solution)/shard_map/reduce_scatter | solution.py:306
  437.2 19.6 %all_to_all.42.refs_0_ = f32[8,2,128,128]{3,2,1,0:T(8,128)} all-to-all(f32[8,2,128,128]{3,2,1,0:T(8,128)} %reduce-scatter.5.cloned.1.call-done), channel_id=1, replica_groups=mesh['depth'=4,'rows'=8] {'rows'}, dimensions={0} | all-to-all | bytes 2097152 | tf_op jit(solution)/shard_map/all_to_all | solution.py:311
  456.8 7.8 %output.1 = f32[2,128,4096]{2,1,0:T(8,128)} custom-call(f32[8,2,128,128]{3,2,1,0:T(8,128)} %all_to_all.42.refs_0_, f32[8,2,128,128]{3,2,1,0:T(8,128)} %copy-done.2, f32[8,2,128,128]{3,2,1,0:T(8,128)} %copy-done.1, f32[8,2,128,128]{3,2,1,0:T(8,128)} %copy-done, f32[32,128]{1,0:T(8,128)} %constant.48.clone.refs_4_, f32[32,128]{1,0:T(8,128)} %constant.49.clone.refs_5_, ...), custom_call_target="tpu_custom_call" | custom-call | flops 1610612736 | bytes 8388608 | tf_op jit(solution)/shard_map/output/pallas_call | solution.py:273
  (20 shorter events, 0.1 us)
Async XLA Ops:
  16.6 6.1 %copy-start.5 = (s32[1,2,4096]{2,1,0:T(2,128)S(1)}, s32[1,2,4096]{2,1,0:T(2,128)}, u32[]{:S(2)}) copy-start(s32[1,2,4096]{2,1,0:T(2,128)} %param.17) | copy-start | bytes 98308
  16.6 54.6 %copy-start.4 = (f32[32,128]{1,0:T(8,128)S(1)}, f32[32,128]{1,0:T(8,128)}, u32[]{:S(2)}) copy-start(f32[32,128]{1,0:T(8,128)} %constant.46.clone.tr_ref) | copy-start | bytes 49156
  16.6 56.5 %copy-start.3 = (f32[32,128]{1,0:T(8,128)S(1)}, f32[32,128]{1,0:T(8,128)}, u32[]{:S(2)}) copy-start(f32[32,128]{1,0:T(8,128)} %constant.47.clone.ti_ref) | copy-start | bytes 49156
  16.6 54.6 %all-to-all-start.6 = ((f32[8,2,512,128]{3,2,1,0:T(8,128)}), f32[8,2,512,128]{3,2,1,0:T(8,128)}, u32[]{:S(2)}, u32[]{:S(2)}) async-start(f32[8,2,512,128]{3,2,1,0:T(8,128)} %width_3.1), calls=%async_computation.9 | async-start | bytes 8388608 | tf_op jit(solution)/shard_map/all_to_all | solution.py:303
  22.0 338.7 %reduce-scatter.11.cloned.1.call-start = ((), (), s32[]{:S(2)}) async-start(), calls=%async_computation.15 | async-start | bytes 5242880 | tf_op jit(solution)/shard_map/reduce_scatter | solution.py:306
  109.0 53.7 %all-to-all-start.4 = ((f32[8,2,512,128]{3,2,1,0:T(8,128)}), f32[8,2,512,128]{3,2,1,0:T(8,128)}, u32[]{:S(2)}, u32[]{:S(2)}) async-start(f32[8,2,512,128]{3,2,1,0:T(8,128)} %width_2.1), calls=%async_computation.6 | async-start | bytes 8388608 | tf_op jit(solution)/shard_map/all_to_all | solution.py:303
  113.6 250.7 %reduce-scatter.9.cloned.1.call-start = ((), (), s32[]{:S(2)}) async-start(), calls=%async_computation.14 | async-start | bytes 5242880 | tf_op jit(solution)/shard_map/reduce_scatter | solution.py:306
  185.9 197.2 %reduce-scatter.7.cloned.1.call-start = ((), (), s32[]{:S(2)}) async-start(), calls=%async_computation.13 | async-start | bytes 5242880 | tf_op jit(solution)/shard_map/reduce_scatter | solution.py:306
  273.4 163.8 %reduce-scatter.5.cloned.1.call-start = ((), (), s32[]{:S(2)}) async-start(), calls=%async_computation.12 | async-start | bytes 5242880 | tf_op jit(solution)/shard_map/reduce_scatter | solution.py:306
  360.7 18.9 %all-to-all-start.7 = ((f32[8,2,128,128]{3,2,1,0:T(8,128)}), f32[8,2,128,128]{3,2,1,0:T(8,128)S(1)}, u32[]{:S(2)}, u32[]{:S(2)}) async-start(f32[8,2,128,128]{3,2,1,0:T(8,128)} %reduce-scatter.11.cloned.1.call-done), calls=%async_computation.11 | async-start | bytes 2097152 | tf_op jit(solution)/shard_map/all_to_all | solution.py:311
  379.6 77.1 %copy-start = (f32[8,2,128,128]{3,2,1,0:T(8,128)}, f32[8,2,128,128]{3,2,1,0:T(8,128)S(1)}, u32[]{:S(2)}) copy-start(f32[8,2,128,128]{3,2,1,0:T(8,128)S(1)} %all-to-all-done.7.refs_3_) | copy-start | bytes 3145732
  379.6 18.9 %all-to-all-start.5 = ((f32[8,2,128,128]{3,2,1,0:T(8,128)}), f32[8,2,128,128]{3,2,1,0:T(8,128)S(1)}, u32[]{:S(2)}, u32[]{:S(2)}) async-start(f32[8,2,128,128]{3,2,1,0:T(8,128)} %reduce-scatter.9.cloned.1.call-done), calls=%async_computation.8 | async-start | bytes 2097152 | tf_op jit(solution)/shard_map/all_to_all | solution.py:311
  398.5 58.3 %copy-start.1 = (f32[8,2,128,128]{3,2,1,0:T(8,128)}, f32[8,2,128,128]{3,2,1,0:T(8,128)S(1)}, u32[]{:S(2)}) copy-start(f32[8,2,128,128]{3,2,1,0:T(8,128)S(1)} %all-to-all-done.5.refs_2_) | copy-start | bytes 3145732
  398.5 38.7 %all-to-all-start.3 = ((f32[8,2,128,128]{3,2,1,0:T(8,128)}), f32[8,2,128,128]{3,2,1,0:T(8,128)S(1)}, u32[]{:S(2)}, u32[]{:S(2)}) async-start(f32[8,2,128,128]{3,2,1,0:T(8,128)} %reduce-scatter.7.cloned.1.call-done), calls=%async_computation.5 | async-start | bytes 2097152 | tf_op jit(solution)/shard_map/all_to_all | solution.py:311
  437.2 19.6 %copy-start.2 = (f32[8,2,128,128]{3,2,1,0:T(8,128)}, f32[8,2,128,128]{3,2,1,0:T(8,128)S(1)}, u32[]{:S(2)}) copy-start(f32[8,2,128,128]{3,2,1,0:T(8,128)S(1)} %all-to-all-done.3.refs_1_) | copy-start | bytes 3145732
Sparse Core Ops, SparseCore 0:
  98.3 76.8 reduce-scatter.10
  186.1 76.6 reduce-scatter.8
  273.6 76.4 reduce-scatter.6
  360.8 76.3 reduce-scatter.4

commit v2 on v1

--- a/solution.py
+++ b/solution.py
@@ -8,6 +8,7 @@
 from jax.experimental import pallas as pl
 from jax.experimental.pallas import tpu as pltpu
 from jax.sharding import PartitionSpec as P
+
 
 LOW = 32
 HIGH = 128
@@ -77,6 +78,11 @@
 def split(value):
     high = value.astype(jnp.bfloat16)
     return high, (value - high.astype(jnp.float32)).astype(jnp.bfloat16)
+
+
+def tripled(value):
+    high, low = split(value)
+    return jnp.concatenate([high, low, high], axis=0)
 
 
 def dot(left, right):
@@ -129,7 +135,6 @@
         scratch_shapes=[pltpu.VMEM((owners, tile, 2 * HIGH), jnp.bfloat16)] * 2,
         compiler_params=pltpu.CompilerParams(vmem_limit_bytes=VMEM_LIMIT),
         cost_estimate=pl.CostEstimate(flops=6 * height * HIGH * HIGH * 4 * owners * 2, bytes_accessed=field.size * 4 + field.size * 4 // chunks, transcendentals=0),
-        name=f"width_{chunk}",
     )(field, *tables)
 
 
@@ -139,8 +144,8 @@
     return [np.float32(c) for c in basis.convert(kind=np.polynomial.Polynomial).coef]
 
 
-COSINE = series(lambda r: np.cos(2.0 * np.pi * r), 8)
-SINE = series(lambda r: np.sin(2.0 * np.pi * r) / r, 8)
+COSINE = series(lambda r: np.cos(2.0 * np.pi * r), 6)
+SINE = series(lambda r: np.sin(2.0 * np.pi * r) / r, 6)
 
 
 def horner(coefficients, at):
@@ -154,7 +159,7 @@
     return jnp.where(natural < N // 2, natural, natural - N).astype(jnp.float32)
 
 
-def column_kernel(scalars_ref, x_ref, tr_ref, ti_ref, fh_ref, fl_ref, ih_ref, il_ref, o_ref, work_ref):
+def column_kernel(scalars_ref, x_ref, tr_ref, ti_ref, f_ref, i_ref, o_ref, work_ref):
     owners, _, pieces, _, _ = x_ref.shape
     distance = scalars_ref[0].astype(jnp.float32) * 2.0 + 100.0
     limit_height = scalars_ref[1].astype(jnp.float32)
@@ -176,7 +181,7 @@
     inside_width = jnp.abs(across) < limit_width
     across_square = (across * (1.0 / N)) ** 2
 
-    def turned(k, sign):
+    def turned(k):
         real, imaginary = work_ref[k, :HIGH, :], work_ref[k, HIGH:, :]
         turn_real, turn_imaginary = tr_ref[k], ti_ref[k]
         return jnp.concatenate(
@@ -186,7 +191,9 @@
     def propagate(k, real, imaginary):
         down = signed(lax.broadcasted_iota(jnp.int32, (HIGH, HIGH), 0) * LOW + k)
         square = (down * (1.0 / N)) ** 2 + across_square
-        turns = -distance * (square / (jnp.sqrt(4.0 - square) + 2.0))
+        rest_square = 4.0 - square
+        drop = 2.0 - rest_square * lax.rsqrt(rest_square)
+        turns = -distance * (0.25 * (square + drop * drop))
         rest = turns - jnp.floor(turns + 0.5)
         at = rest * rest
         keep = jnp.logical_and(jnp.abs(down) < limit_height, inside_width)
@@ -196,14 +203,12 @@
 
     def middle(step, carry):
         pair = [2 * step, 2 * step + 1]
-        high, low = split(jnp.concatenate([turned(k, 1.0) for k in pair], axis=1))
-        spectrum = dot(fh_ref[...], high) + dot(fh_ref[...], low) + dot(fl_ref[...], high)
+        spectrum = dot(f_ref[...], tripled(jnp.concatenate([turned(k) for k in pair], axis=1)))
         moved = [
             propagate(k, spectrum[:HIGH, i * HIGH:(i + 1) * HIGH], spectrum[HIGH:, i * HIGH:(i + 1) * HIGH])
             for i, k in enumerate(pair)
         ]
-        high, low = split(jnp.concatenate(moved, axis=1))
-        back = dot(ih_ref[...], high) + dot(ih_ref[...], low) + dot(il_ref[...], high)
+        back = dot(i_ref[...], tripled(jnp.concatenate(moved, axis=1)))
         for i, k in enumerate(pair):
             real, imaginary = back[:HIGH, i * HIGH:(i + 1) * HIGH], back[HIGH:, i * HIGH:(i + 1) * HIGH]
             turn_real, turn_imaginary = tr_ref[k], ti_ref[k]
@@ -225,7 +230,7 @@
     lax.fori_loop(0, HIGH // 8, inverse, 0)
 
 
-def columns_step(received, scalars, tables, chunk):
+def columns_step(received, scalars, tables):
     owners, _, height, _ = received.shape
     received = received.reshape(owners, 2, height // HIGH, HIGH, HIGH)
     vmem = pl.BlockSpec(memory_space=pltpu.VMEM)
@@ -237,7 +242,6 @@
         scratch_shapes=[pltpu.VMEM((LOW, 2 * HIGH, HIGH), jnp.float32)],
         compiler_params=pltpu.CompilerParams(vmem_limit_bytes=VMEM_LIMIT),
         cost_estimate=pl.CostEstimate(flops=12 * LOW * HIGH * 256 * 256 * 2, bytes_accessed=16 * 1024 * 1024, transcendentals=0),
-        name=f"column_{chunk}",
     )(scalars, received, *tables)
 
 
@@ -288,7 +292,7 @@
     field = target.reshape(target.shape[1:])
     scale = 1.0 / math.sqrt(N)
     forward, backward = dense_table(-1.0), dense_table(1.0)
-    forward_left, backward_left = halves(forward), halves(backward)
+    left = tuple(jnp.concatenate([h, h, l], axis=1) for h, l in (halves(forward), halves(backward)))
     forward_right, backward_right = halves(forward.T), halves(backward.T)
     turn = twiddles(-1.0, scale)
     turn_back = twiddles(1.0, scale / math.sqrt(depths))
@@ -302,7 +306,7 @@
         sent = along_width(field, chunk, chunks, owners, turn + forward_right)
         received = lax.all_to_all(sent, "rows", split_axis=0, concat_axis=0, tiled=True)
         scalars = jnp.stack([depth_index[0], limits[0], limits[1], me * chunks + chunk]).astype(jnp.int32)
-        part = columns_step(received, scalars, spread + forward_left + backward_left, chunk)
+        part = columns_step(received, scalars, spread + left)
         pieces.append(lax.psum_scatter(part, "depth", scatter_dimension=0, tiled=True))
     results = []
     for share in pieces:

time: 472 us -> 468 us (level)
  transfers between devices with their start and end apart: 9 -> 9, of which waited for: 5 -> 5; matrix products, arithmetic and copies ran while one was open for 0% -> 0% of each run, Pallas kernels for 22% -> 21%
where the time goes in v2:
time: 468 us; the launch traced here: 467 us
  waiting for transfers between devices  162 us (35%)
  Pallas kernels  139 us (30%)
  blocking collectives  127 us (27%)
  starting transfers between devices  20.8 us (4%)
  between operations  13.9 us (3%)
    all_to_all x2, blocking collectives, local(): lax.all_to_all(sent, 'rows', split_axis=0, concat_axis=0, tiled=True)  107 us
    all_to_all x2, waiting for transfers between devices, local(): lax.all_to_all(sent, 'rows', split_axis=0, concat_axis=0, tiled=True)  96.1 us
    pallas_call x4, Pallas kernels, columns_step(): pl.pallas_call(column_kernel, in_specs=[pl.BlockSpec(memory_space=pltpu.S...  89.3 us
    pallas_call x4, Pallas kernels, along_width(): pl.pallas_call(functools.partial(width_kernel, chunk, chunks, owners), gr...  41.8 us
    reduce_scatter x4, waiting for transfers between devices, local(): lax.psum_scatter(part, 'depth', scatter_dimension=0, tiled=True)  35.2 us
    all_to_all x3, waiting for transfers between devices, local(): lax.all_to_all(share, 'rows', split_axis=0, concat_axis=0, tiled=True)  30.6 us
    all_to_all x1, blocking collectives, local(): lax.all_to_all(share, 'rows', split_axis=0, concat_axis=0, tiled=True)  19.6 us
    all_to_all x3, starting transfers between devices, local(): lax.all_to_all(share, 'rows', split_axis=0, concat_axis=0, tiled=True)  10.7 us
  transfers between devices with their start and end apart: 9, of which 5 were waited for; matrix products, arithmetic and copies ran while one was open for 0% of the time, Pallas kernels for 21%

profile of v2, /device:TPU:0, one launch (start us, length us, event | category | flops | bytes accessed | tf_op | source)
XLA Modules:
  0.0 467.4 jit_solution(16929111448793908546)
XLA Ops:
  6.5 10.1 %shard_map.151 = f32[8,2,512,128]{3,2,1,0:T(8,128)} custom-call(f32[2,512,4096]{2,1,0:T(8,128)} %bitcast.9, f32[32,128]{1,0:T(8,128)} %constant.46.clone.tr_ref, f32[32,128]{1,0:T(8,128)} %constant.47.clone.ti_ref, bf16[256,256]{1,0:T(8,128)(2,1)} %constant.44.clone.th_ref, bf16[256,256]{1,0:T(8,128)(2,1)} %constant.45.clone.tl_ref), custom_call_target="tpu_custom_call" | custom-call | flops 3221225472 | bytes 20971520 | tf_op jit(solution)/shard_map/pallas_call | solution.py:129
  16.6 5.3 %all-to-all-start.6 = ((f32[8,2,512,128]{3,2,1,0:T(8,128)}), f32[8,2,512,128]{3,2,1,0:T(8,128)}, u32[]{:S(2)}, u32[]{:S(2)}) async-start(f32[8,2,512,128]{3,2,1,0:T(8,128)} %shard_map.151), calls=%async_computation.9 | async-start | bytes 8388608 | tf_op jit(solution)/shard_map/all_to_all | solution.py:307
  22.0 0.0 reduce-scatter.11.cloned.1.call-start
  22.7 0.2 reduce_sum.9
  22.8 0.7 pad_add_fusion.4
  23.5 47.7 %all-to-all-done.6 = f32[8,2,512,128]{3,2,1,0:T(8,128)} async-done(((f32[8,2,512,128]{3,2,1,0:T(8,128)}), f32[8,2,512,128]{3,2,1,0:T(8,128)}, u32[]{:S(2)}, u32[]{:S(2)}) %all-to-all-start.6) | async-done | bytes 4194336 | tf_op jit(solution)/shard_map/all_to_all | solution.py:307
  71.2 1.9 broadcast_in_dim.4.tr_ref
  73.1 1.9 broadcast_in_dim.5.ti_ref
  75.0 22.2 %shard_map.152 = f32[32,2,128,128]{3,2,1,0:T(8,128)} custom-call(s32[4]{0:T(128)} %get-tuple-element.5.scalars_ref, f32[8,2,4,128,128]{4,3,2,1,0:T(8,128)} %bitcast.8.x_ref, f32[32,128,128]{2,1,0:T(8,128)} %broadcast_in_dim.4.tr_ref, f32[32,128,128]{2,1,0:T(8,128)} %broadcast_in_dim.5.ti_ref, bf16[256,768]{1,0:T(8,128)(2,1)} %constant.53.f_ref, ...), custom_call_target="tpu_custom_call" | custom-call | flops 6442450944 | bytes 16777216 | tf_op jit(solution)/shard_map/pallas_call | solution.py:237
  97.3 10.8 %shard_map.149 = f32[8,2,512,128]{3,2,1,0:T(8,128)} custom-call(f32[2,512,4096]{2,1,0:T(8,128)} %bitcast.10, f32[32,128]{1,0:T(8,128)} %constant.46.clone.tr_ref, f32[32,128]{1,0:T(8,128)} %constant.47.clone.ti_ref, bf16[256,256]{1,0:T(8,128)(2,1)} %constant.44.clone.th_ref, bf16[256,256]{1,0:T(8,128)(2,1)} %constant.45.clone.tl_ref), custom_call_target="tpu_custom_call" | custom-call | flops 3221225472 | bytes 20971520 | tf_op jit(solution)/shard_map/pallas_call | solution.py:129
  108.1 4.6 all-to-all-start.4
  112.7 0.0 reduce-scatter.9.cloned.1.call-start
  112.7 0.7 pad_add_fusion.3
  113.4 48.4 %all-to-all-done.4 = f32[8,2,512,128]{3,2,1,0:T(8,128)} async-done(((f32[8,2,512,128]{3,2,1,0:T(8,128)}), f32[8,2,512,128]{3,2,1,0:T(8,128)}, u32[]{:S(2)}, u32[]{:S(2)}) %all-to-all-start.4) | async-done | bytes 4194336 | tf_op jit(solution)/shard_map/all_to_all | solution.py:307
  161.8 22.3 %shard_map.150 = f32[32,2,128,128]{3,2,1,0:T(8,128)} custom-call(s32[4]{0:T(128)} %get-tuple-element.7.scalars_ref, f32[8,2,4,128,128]{4,3,2,1,0:T(8,128)} %bitcast.6.x_ref, f32[32,128,128]{2,1,0:T(8,128)} %broadcast_in_dim.4.tr_ref, f32[32,128,128]{2,1,0:T(8,128)} %broadcast_in_dim.5.ti_ref, bf16[256,768]{1,0:T(8,128)(2,1)} %constant.53.f_ref, ...), custom_call_target="tpu_custom_call" | custom-call | flops 6442450944 | bytes 16777216 | tf_op jit(solution)/shard_map/pallas_call | solution.py:237
  184.1 0.0 reduce-scatter.7.cloned.1.call-start
  184.2 10.6 %shard_map.147 = f32[8,2,512,128]{3,2,1,0:T(8,128)} custom-call(f32[2,512,4096]{2,1,0:T(8,128)} %bitcast.11, f32[32,128]{1,0:T(8,128)} %constant.46.clone.tr_ref, f32[32,128]{1,0:T(8,128)} %constant.47.clone.ti_ref, bf16[256,256]{1,0:T(8,128)(2,1)} %constant.44.clone.th_ref, bf16[256,256]{1,0:T(8,128)(2,1)} %constant.45.clone.tl_ref), custom_call_target="tpu_custom_call" | custom-call | flops 3221225472 | bytes 20971520 | tf_op jit(solution)/shard_map/pallas_call | solution.py:129
  194.8 53.5 %all_to_all.40 = f32[8,2,512,128]{3,2,1,0:T(8,128)} all-to-all(f32[8,2,512,128]{3,2,1,0:T(8,128)} %shard_map.147), channel_id=1, replica_groups=mesh['depth'=4,'rows'=8] {'rows'}, dimensions={0} | all-to-all | bytes 8388608 | tf_op jit(solution)/shard_map/all_to_all | solution.py:307
  248.4 22.3 %shard_map.148 = f32[32,2,128,128]{3,2,1,0:T(8,128)} custom-call(s32[4]{0:T(128)} %get-tuple-element.8.scalars_ref, f32[8,2,4,128,128]{4,3,2,1,0:T(8,128)} %bitcast.14, f32[32,128,128]{2,1,0:T(8,128)} %broadcast_in_dim.4.tr_ref, f32[32,128,128]{2,1,0:T(8,128)} %broadcast_in_dim.5.ti_ref, bf16[256,768]{1,0:T(8,128)(2,1)} %constant.53.f_ref, ...), custom_call_target="tpu_custom_call" | custom-call | flops 6442450944 | bytes 16777216 | tf_op jit(solution)/shard_map/pallas_call | solution.py:237
  270.7 0.0 reduce-scatter.5.cloned.1.call-start
  270.8 10.3 %shard_map.145 = f32[8,2,512,128]{3,2,1,0:T(8,128)} custom-call(f32[2,512,4096]{2,1,0:T(8,128)} %bitcast.12, f32[32,128]{1,0:T(8,128)} %constant.46.clone.tr_ref, f32[32,128]{1,0:T(8,128)} %constant.47.clone.ti_ref, bf16[256,256]{1,0:T(8,128)(2,1)} %constant.44.clone.th_ref, bf16[256,256]{1,0:T(8,128)(2,1)} %constant.45.clone.tl_ref), custom_call_target="tpu_custom_call" | custom-call | flops 3221225472 | bytes 20971520 | tf_op jit(solution)/shard_map/pallas_call | solution.py:129
  281.1 53.5 %all_to_all.41 = f32[8,2,512,128]{3,2,1,0:T(8,128)} all-to-all(f32[8,2,512,128]{3,2,1,0:T(8,128)} %shard_map.145), channel_id=1, replica_groups=mesh['depth'=4,'rows'=8] {'rows'}, dimensions={0} | all-to-all | bytes 8388608 | tf_op jit(solution)/shard_map/all_to_all | solution.py:307
  334.6 22.4 %shard_map.146 = f32[32,2,128,128]{3,2,1,0:T(8,128)} custom-call(s32[4]{0:T(128)} %get-tuple-element.9.scalars_ref, f32[8,2,4,128,128]{4,3,2,1,0:T(8,128)} %bitcast.13, f32[32,128,128]{2,1,0:T(8,128)} %broadcast_in_dim.4.tr_ref, f32[32,128,128]{2,1,0:T(8,128)} %broadcast_in_dim.5.ti_ref, bf16[256,768]{1,0:T(8,128)(2,1)} %constant.53.f_ref, ...), custom_call_target="tpu_custom_call" | custom-call | flops 6442450944 | bytes 16777216 | tf_op jit(solution)/shard_map/pallas_call | solution.py:237
  357.1 3.6 all-to-all-start.7
  360.7 15.3 %all-to-all-done.7.refs_3_ = f32[8,2,128,128]{3,2,1,0:T(8,128)S(1)} async-done(((f32[8,2,128,128]{3,2,1,0:T(8,128)}), f32[8,2,128,128]{3,2,1,0:T(8,128)S(1)}, u32[]{:S(2)}, u32[]{:S(2)}) %all-to-all-start.7) | async-done | bytes 1048608 | tf_op jit(solution)/shard_map/all_to_all | solution.py:315
  376.0 3.6 all-to-all-start.5
  379.5 0.0 reduce-scatter.7.cloned.1.call-done
  379.5 15.3 %all-to-all-done.5.refs_2_ = f32[8,2,128,128]{3,2,1,0:T(8,128)S(1)} async-done(((f32[8,2,128,128]{3,2,1,0:T(8,128)}), f32[8,2,128,128]{3,2,1,0:T(8,128)S(1)}, u32[]{:S(2)}, u32[]{:S(2)}) %all-to-all-start.5) | async-done | bytes 1048608 | tf_op jit(solution)/shard_map/all_to_all | solution.py:315
  394.8 3.6 all-to-all-start.3
  398.4 35.1 %reduce-scatter.5.cloned.1.call-done = f32[8,2,128,128]{3,2,1,0:T(8,128)} async-done(((f32[32,2,128,128]{3,2,1,0:T(8,128)}), f32[8,2,128,128]{3,2,1,0:T(8,128)}) %reduce-scatter.5.cloned.1.call-update) | async-done | bytes 1048592 | tf_op jit(solution)/shard_map/reduce_scatter | solution.py:310
  433.5 19.6 %all_to_all.42.refs_0_ = f32[8,2,128,128]{3,2,1,0:T(8,128)} all-to-all(f32[8,2,128,128]{3,2,1,0:T(8,128)} %reduce-scatter.5.cloned.1.call-done), channel_id=1, replica_groups=mesh['depth'=4,'rows'=8] {'rows'}, dimensions={0} | all-to-all | bytes 2097152 | tf_op jit(solution)/shard_map/all_to_all | solution.py:315
  453.1 7.8 %output.1 = f32[2,128,4096]{2,1,0:T(8,128)} custom-call(f32[8,2,128,128]{3,2,1,0:T(8,128)} %all_to_all.42.refs_0_, f32[8,2,128,128]{3,2,1,0:T(8,128)} %copy-done.2, f32[8,2,128,128]{3,2,1,0:T(8,128)} %copy-done.1, f32[8,2,128,128]{3,2,1,0:T(8,128)} %copy-done, f32[32,128]{1,0:T(8,128)} %constant.48.clone.refs_4_, f32[32,128]{1,0:T(8,128)} %constant.49.clone.refs_5_, ...), custom_call_target="tpu_custom_call" | custom-call | flops 1610612736 | bytes 8388608 | tf_op jit(solution)/shard_map/output/pallas_call | solution.py:277
  (20 shorter events, 0.1 us)
Async XLA Ops:
  16.6 6.1 %copy-start.5 = (s32[1,2,4096]{2,1,0:T(2,128)S(1)}, s32[1,2,4096]{2,1,0:T(2,128)}, u32[]{:S(2)}) copy-start(s32[1,2,4096]{2,1,0:T(2,128)} %param.17) | copy-start | bytes 98308
  16.6 54.6 %copy-start.4 = (f32[32,128]{1,0:T(8,128)S(1)}, f32[32,128]{1,0:T(8,128)}, u32[]{:S(2)}) copy-start(f32[32,128]{1,0:T(8,128)} %constant.46.clone.tr_ref) | copy-start | bytes 49156
  16.6 56.5 %copy-start.3 = (f32[32,128]{1,0:T(8,128)S(1)}, f32[32,128]{1,0:T(8,128)}, u32[]{:S(2)}) copy-start(f32[32,128]{1,0:T(8,128)} %constant.47.clone.ti_ref) | copy-start | bytes 49156
  16.6 54.6 %all-to-all-start.6 = ((f32[8,2,512,128]{3,2,1,0:T(8,128)}), f32[8,2,512,128]{3,2,1,0:T(8,128)}, u32[]{:S(2)}, u32[]{:S(2)}) async-start(f32[8,2,512,128]{3,2,1,0:T(8,128)} %shard_map.151), calls=%async_computation.9 | async-start | bytes 8388608 | tf_op jit(solution)/shard_map/all_to_all | solution.py:307
  22.0 335.1 %reduce-scatter.11.cloned.1.call-start = ((), (), s32[]{:S(2)}) async-start(), calls=%async_computation.15 | async-start | bytes 5242880 | tf_op jit(solution)/shard_map/reduce_scatter | solution.py:310
  108.1 53.7 %all-to-all-start.4 = ((f32[8,2,512,128]{3,2,1,0:T(8,128)}), f32[8,2,512,128]{3,2,1,0:T(8,128)}, u32[]{:S(2)}, u32[]{:S(2)}) async-start(f32[8,2,512,128]{3,2,1,0:T(8,128)} %shard_map.149), calls=%async_computation.6 | async-start | bytes 8388608 | tf_op jit(solution)/shard_map/all_to_all | solution.py:307
  112.7 248.0 %reduce-scatter.9.cloned.1.call-start = ((), (), s32[]{:S(2)}) async-start(), calls=%async_computation.14 | async-start | bytes 5242880 | tf_op jit(solution)/shard_map/reduce_scatter | solution.py:310
  184.1 195.4 %reduce-scatter.7.cloned.1.call-start = ((), (), s32[]{:S(2)}) async-start(), calls=%async_computation.13 | async-start | bytes 5242880 | tf_op jit(solution)/shard_map/reduce_scatter | solution.py:310
  270.7 162.8 %reduce-scatter.5.cloned.1.call-start = ((), (), s32[]{:S(2)}) async-start(), calls=%async_computation.12 | async-start | bytes 5242880 | tf_op jit(solution)/shard_map/reduce_scatter | solution.py:310
  357.1 18.9 %all-to-all-start.7 = ((f32[8,2,128,128]{3,2,1,0:T(8,128)}), f32[8,2,128,128]{3,2,1,0:T(8,128)S(1)}, u32[]{:S(2)}, u32[]{:S(2)}) async-start(f32[8,2,128,128]{3,2,1,0:T(8,128)} %reduce-scatter.11.cloned.1.call-done), calls=%async_computation.11 | async-start | bytes 2097152 | tf_op jit(solution)/shard_map/all_to_all | solution.py:315
  376.0 77.2 %copy-start = (f32[8,2,128,128]{3,2,1,0:T(8,128)}, f32[8,2,128,128]{3,2,1,0:T(8,128)S(1)}, u32[]{:S(2)}) copy-start(f32[8,2,128,128]{3,2,1,0:T(8,128)S(1)} %all-to-all-done.7.refs_3_) | copy-start | bytes 3145732
  376.0 18.9 %all-to-all-start.5 = ((f32[8,2,128,128]{3,2,1,0:T(8,128)}), f32[8,2,128,128]{3,2,1,0:T(8,128)S(1)}, u32[]{:S(2)}, u32[]{:S(2)}) async-start(f32[8,2,128,128]{3,2,1,0:T(8,128)} %reduce-scatter.9.cloned.1.call-done), calls=%async_computation.8 | async-start | bytes 2097152 | tf_op jit(solution)/shard_map/all_to_all | solution.py:315
  394.8 58.3 %copy-start.1 = (f32[8,2,128,128]{3,2,1,0:T(8,128)}, f32[8,2,128,128]{3,2,1,0:T(8,128)S(1)}, u32[]{:S(2)}) copy-start(f32[8,2,128,128]{3,2,1,0:T(8,128)S(1)} %all-to-all-done.5.refs_2_) | copy-start | bytes 3145732
  394.8 38.7 %all-to-all-start.3 = ((f32[8,2,128,128]{3,2,1,0:T(8,128)}), f32[8,2,128,128]{3,2,1,0:T(8,128)S(1)}, u32[]{:S(2)}, u32[]{:S(2)}) async-start(f32[8,2,128,128]{3,2,1,0:T(8,128)} %reduce-scatter.7.cloned.1.call-done), calls=%async_computation.5 | async-start | bytes 2097152 | tf_op jit(solution)/shard_map/all_to_all | solution.py:315
  433.5 19.6 %copy-start.2 = (f32[8,2,128,128]{3,2,1,0:T(8,128)}, f32[8,2,128,128]{3,2,1,0:T(8,128)S(1)}, u32[]{:S(2)}) copy-start(f32[8,2,128,128]{3,2,1,0:T(8,128)S(1)} %all-to-all-done.3.refs_1_) | copy-start | bytes 3145732
Sparse Core Ops, SparseCore 0:
  97.4 76.8 reduce-scatter.10
  184.2 76.6 reduce-scatter.8
  270.8 76.4 reduce-scatter.6
  357.2 76.3 reduce-scatter.4
